TPU v7x, 32 devices: a whole 2x2x4 slice. The times are simulated.
32 devices in a mesh: row: 4 (over y, x), col: 8 (over z, core).
Axes of the slice: x: 2, y: 2, z: 4, core: 2. Of those that a mesh axis runs over, the one named last changes fastest.
Arguments:
- basis_values: bfloat16 [8, 4, 4096, 256], P('col', 'row'), may hold values from -6 to 6
- weights: float32 [8, 4, 4096], P('col', 'row'), may hold values from 0.00390625 to 0.03125
- kernel: float32 [8, 4, 4096], P('col', 'row'), may hold values from -2 to -0.25
- live_points: int32 [8, 4], P('col', 'row'), may hold values from 1024 to 4096
- batch_tiles: int32 [8, 4, 2], P('col', 'row'), may hold values from 0 to 31, as said below
- density: bfloat16 [8, 4, 2, 2, 128, 128], P('col', 'row'), may hold values from -0.03125 to 0.03125
- tile_lists: int32 [8, 4, 2], P('col', 'row'), may hold values from 0 to 31, as said below
Outputs:
- hamiltonian: float32 [8, 4, 2, 2, 128, 128], P('col', 'row')
Inputs may be any that keep to these rules, and one draw needn't show every extreme that they name: `batch_tiles`: tile t belongs to column t // 4. The first tile of the batch on column c belongs to column c, and each tile is the first tile of exactly one batch; the second tile differs from the first and belongs to column c - 1, c or c + 1, taken cyclically over 8 columns. `tile_lists`: each tile row of column c is held by exactly one device of column c, and its list starts with the row itself. The list of tile row t equals the list of the batch whose first tile is t.
All inputs are finite; a program needn't handle non-finite values.
Results may differ from a plain program's by a relative error of at most 0.0044.
Values may be sent and summed in bfloat16 or wider, within the bound.
No kernel may reach another device: no remote copies, remote signals or barrier semaphores. Data moves between devices by JAX's collectives and lax.ppermute only.
A program may use at most 64 MiB of HBM per device.

v0:
```python
import jax
import jax.numpy as jnp
from jax import lax
from jax.sharding import PartitionSpec as P


def padded(cells, sides, width):
    for axis, dim in sides:
        count = lax.axis_size(axis)
        head = lax.slice_in_dim(cells, 0, width, axis=dim)
        tail = lax.slice_in_dim(cells, cells.shape[dim] - width, cells.shape[dim], axis=dim)
        cells = jnp.concatenate(
            [
                lax.ppermute(tail, axis, [(i, (i + 1) % count) for i in range(count)]),
                cells,
                lax.ppermute(head, axis, [((i + 1) % count, i) for i in range(count)]),
            ],
            axis=dim,
        )
    return cells


def passed_along(block, axis, distance):
    devices = range(lax.axis_size(axis))
    route = [((i - distance) % len(devices), i) for i in devices]
    return lax.ppermute(block, axis, route)


def pair_ids(listed):
    head = listed[..., 0]
    tail = listed[..., 1]
    pair_rows = jnp.stack([head, head, tail, tail], -1)
    pair_cols = jnp.stack([head, tail, head, tail], -1)
    return (pair_rows, pair_cols)


def pick_tiles(pair_rows, pair_cols, tiles, tile_rows, tile_cols):
    matched = (pair_rows[:, None] == tile_rows[None, :]) & (
        pair_cols[:, None] == tile_cols[None, :]
    )
    table = matched.astype(jnp.bfloat16)
    flat_tiles = tiles.reshape(tiles.shape[0], -1)
    picked = jnp.dot(table, flat_tiles, preferred_element_type=jnp.float32).astype(jnp.bfloat16)
    return picked.reshape((pair_rows.shape[0],) + tiles.shape[1:])


def response(values, weight_row, kernel_row, live_count, tiles):
    points, basis = values.shape
    width = tiles.shape[-1]
    upper_half = jnp.concatenate([tiles[0], tiles[1]], 2)
    lower_half = jnp.concatenate([tiles[2], tiles[3]], 2)
    local = jnp.concatenate([upper_half, lower_half], 1)
    joined = jnp.concatenate([local[0], local[1]], 1)
    projected = jnp.dot(values, joined, preferred_element_type=jnp.float32)
    density_one = jnp.sum(projected[:, :basis] * values, axis=1)
    density_two = jnp.sum(projected[:, basis:] * values, axis=1)
    alive = (jnp.arange(points, dtype=jnp.int32) < live_count).astype(jnp.float32)
    factor = alive * weight_row * kernel_row
    scaled = jnp.concatenate(
        [
            ((factor * density_one)[:, None] * values).astype(jnp.bfloat16),
            ((factor * density_two)[:, None] * values).astype(jnp.bfloat16),
        ],
        1,
    )
    hamilton = lax.dot_general(
        values, scaled, (((0,), (0,)), ((), ())), preferred_element_type=jnp.float32
    )
    blocks = []
    for left_index in (0, 1):
        for right_index in (0, 1):
            per_pert = []
            for pert_index in (0, 1):
                start_col = pert_index * basis + right_index * width
                per_pert.append(
                    hamilton[
                        left_index * width : (left_index + 1) * width, start_col : start_col + width
                    ]
                )
            blocks.append(jnp.stack(per_pert))
    return jnp.stack(blocks)


def on_device(basis_values, weights, kernel, live_points, batch_tiles, density, tile_lists):
    row_count = lax.axis_size("row")
    list_len = tile_lists.shape[2]
    tile_shape = density.shape[3:]
    density_col, lists_col = (
        lax.all_gather(density, "row", axis=1, tiled=True),
        lax.all_gather(tile_lists, "row", axis=1, tiled=True),
    )
    column_slots = row_count * list_len
    key_rows = jnp.concatenate(
        [lists_col.reshape(1, column_slots), batch_tiles.reshape(1, list_len)], 1
    )
    band_keys = padded(key_rows, (("col", 0),), 1)
    band_batches = band_keys[:, column_slots:]
    column_rows = jnp.broadcast_to(lists_col[0, :, :1], (row_count, list_len)).reshape(column_slots)
    column_cols = lists_col[0].reshape(column_slots)
    lower_rows, lower_cols = pair_ids(band_batches[0])
    own_rows, own_cols = pair_ids(band_batches[1])
    upper_rows, upper_cols = pair_ids(band_batches[2])
    column_tiles = density_col.reshape((column_slots,) + tile_shape)
    for_lower = pick_tiles(lower_rows, lower_cols, column_tiles, column_rows, column_cols)
    for_upper = pick_tiles(upper_rows, upper_cols, column_tiles, column_rows, column_cols)
    from_upper = passed_along(for_lower, "col", -1)
    from_lower = passed_along(for_upper, "col", 1)
    tiles = (
        pick_tiles(own_rows, own_cols, column_tiles, column_rows, column_cols)
        + from_upper
        + from_lower
    )
    partial_value = response(
        basis_values[0, 0], weights[0, 0], kernel[0, 0], live_points[0, 0], tiles
    )
    sums_lower = passed_along(partial_value, "col", 1)
    sums_upper = passed_along(partial_value, "col", -1)
    entries = jnp.concatenate([partial_value, sums_lower, sums_upper], 0)
    entry_rows = jnp.concatenate([own_rows, lower_rows, upper_rows], 0)
    entry_cols = jnp.concatenate([own_cols, lower_cols, upper_cols], 0)
    matched = (
        (column_rows[:, None] == entry_rows[None, :])
        & (column_cols[:, None] == entry_cols[None, :])
    ).astype(jnp.float32)
    term = jnp.dot(
        matched,
        entries.reshape(entries.shape[0], -1),
        precision=lax.Precision.HIGHEST,
        preferred_element_type=jnp.float32,
    )
    term = term.reshape((row_count, list_len) + tile_shape)
    owned = lax.psum_scatter(term, "row", scatter_dimension=0, tiled=True)
    return owned.reshape((1, 1, list_len) + tile_shape)


def solution(mesh):
    placed = (
        P("col", "row", None, None),
        P("col", "row", None),
        P("col", "row", None),
        P("col", "row"),
        P("col", "row", None),
        P("col", "row", None, None, None, None),
        P("col", "row", None),
    )
    return jax.shard_map(
        on_device,
        mesh=mesh,
        in_specs=placed,
        out_specs=P("col", "row", None, None, None, None),
        check_vma=False,
    )
```

profile of v0, /device:TPU:0, one launch (start us, length us, event | category | flops | bytes accessed | tf_op | source)
XLA Modules:
  0.0 112.1 jit_solution(13996948292295933413)
XLA Ops:
  6.5 9.5 %all_gather.6 = s32[1,4,2]{2,0,1:T(1,128)S(1)} all-gather(s32[1,1,2]{2,0,1:T(1,128)} %bitcast.140), channel_id=1, replica_groups=mesh['row'=4,'col'=8] {'row'}, dimensions={1}, use_global_device_ids=true | all-gather | bytes 40 | tf_op jit(solution)/shard_map/all_gather | solution.py:90
  16.1 0.5 broadcast.66
  16.6 0.7 reduce.7
  17.2 0.1 reshape.104
  17.3 0.7 pad_add_fusion
  18.1 3.5 %collective-permute-start.1 = (s32[1,10]{1,0:T(1,128)S(1)}, s32[1,10]{1,0:T(1,128)S(1)}, u32[]{:S(2)}, u32[]{:S(2)}) collective-permute-start(s32[1,10]{1,0:T(1,128)S(1)} %pad_add_fusion), channel_id=1, source_target_pairs={{1,0},{2,1},{3,2},{4,3},{5,4},{6,5},{7,6},{0,7},{9,8},{10,9},{11,1... | collective-permute-start | bytes 128 | tf_op jit(solution)/shard_map/ppermute | solution.py:16
  21.6 0.2 slice_reduce_fusion
  21.8 0.1 broadcast_in_dim.5
  21.8 0.1 eq.120
  21.9 0.1 eq.124
  22.0 10.7 %all_gather.7 = bf16[1,4,2,2,128,128]{5,4,3,2,0,1:T(8,128)(2,1)S(1)} all-gather(bf16[1,1,2,2,128,128]{5,4,3,2,0,1:T(8,128)(2,1)} %bitcast.133), channel_id=1, replica_groups=mesh['row'=4,'col'=8] {'row'}, dimensions={1}, use_global_device_ids=true | all-gather | bytes 655360 | tf_op jit(solution)/shard_map/all_gather | solution.py:89
  32.7 0.2 reshape_reshape.2
  33.0 0.7 fusion.61
  33.7 1.3 %add_add_fusion.3 = (s32[4]{0:T(128)S(1)}, s32[4]{0:T(128)S(1)}) fusion(s32[1]{0:T(128)} %bitcast.5, s32[1]{0:T(128)} %bitcast.4), kind=kLoop, calls=%fused_computation.88 | loop fusion | flops 24 | bytes 40 | tf_op jit(solution)/shard_map/stack | solution.py:32
  35.0 0.4 fusion.19
  35.4 0.1 collective-permute-start.2
  35.4 0.6 fusion.63
  36.1 1.3 %add_add_fusion.5 = (s32[4]{0:T(128)S(1)}, s32[4]{0:T(128)S(1)}) fusion(s32[1]{0:T(128)} %bitcast.7, s32[1]{0:T(128)} %bitcast.6), kind=kLoop, calls=%fused_computation.90 | loop fusion | flops 24 | bytes 40 | tf_op jit(solution)/shard_map/stack | solution.py:32
  37.4 0.4 fusion.20
  37.8 0.5 collective-permute-start.3
  38.4 0.6 fusion.62
  39.0 1.3 %add_add_fusion.1 = (s32[4]{0:T(128)S(1)}, s32[4]{0:T(128)S(1)}) fusion(s32[1]{0:T(128)} %bitcast.3, s32[1]{0:T(128)} %bitcast.2), kind=kLoop, calls=%fused_computation.86 | loop fusion | flops 24 | bytes 40 | tf_op jit(solution)/shard_map/stack | solution.py:32
  40.3 0.4 fusion.18
  40.8 2.9 %copy.22 = bf16[1,1,4096,256]{2,3,1,0:T(8,128)(2,1)S(1)} copy(bf16[1,1,4096,256]{3,2,1,0:T(8,128)(2,1)} %param.7) | data formatting | bytes 4194304 | tf_op args[0]
  44.5 1.0 collective-permute-done.3
  45.6 1.3 %convolution_bitcast_fusion = f32[4096,512]{0,1:T(8,128)S(1)} fusion(bf16[1,1,4096,256]{3,2,1,0:T(8,128)(2,1)S(1)} %copy-done, bf16[256,256]{1,0:T(8,128)(2,1)S(1)} %get-tuple-element.18, bf16[256,256]{1,0:T(8,128)(2,1)S(1)} %get-tuple-element.17), kind=kOutput, calls=%fused_computation.7 | convolution fusion | flops 1074266112 | bytes 10747904 | tf_op jit(solution)/shard_map/dot_general | solution.py:54
  47.0 1.1 fusion
  48.1 0.9 fusion.1
  49.0 1.3 %fusion.13 = f32[256,512]{0,1:T(8,128)S(1)} fusion(bf16[1,1,4096,256]{3,2,1,0:T(8,128)(2,1)S(1)} %copy-done, bf16[4096,256]{0,1:T(8,128)(2,1)S(1)} %get-tuple-element.8, bf16[4096,256]{0,1:T(8,128)(2,1)S(1)} %get-tuple-element.7), kind=kOutput, calls=%fused_computation.21 | convolution fusion | flops 1082130432 | bytes 6815744 | tf_op jit(solution)/shard_map/dot_general | solution.py:66
  50.4 2.8 %collective-permute-start.5 = (f32[4,2,128,128]{2,3,1,0:T(8,128)S(1)}, f32[4,2,128,128]{2,3,1,0:T(8,128)S(1)}, u32[]{:S(2)}, u32[]{:S(2)}) collective-permute-start(f32[4,2,128,128]{2,3,1,0:T(8,128)S(1)} %pad_maximum_fusion), channel_id=1, source_target_pairs={{1,0},{2,1},{3,2},{4,3},{5,4},{6,5},{7,6},{0,7},{9,8},{10,9},{11,1... | collective-permute-start | bytes 1572872 | tf_op jit(solution)/shard_map/ppermute | solution.py:26
  53.2 0.1 copy.20
  53.3 7.6 %concatenate.45 = s32[12]{0:T(128)S(1)} concatenate(s32[1]{0:T(128)} %bitcast.2, s32[1]{0:T(128)} %bitcast.2, s32[1]{0:T(128)} %bitcast.3, s32[1]{0:T(128)} %bitcast.3, s32[1]{0:T(128)} %bitcast.4, s32[1]{0:T(128)} %bitcast.4, s32[1]{0:T(128)} %bitcast.5, s32[1]{0:T(128)} %bitcast.5, s32[1]{0:T(128)} %bitcast.6, s32[1]{0:T(128)} %bitcast.6, s32[1]{0:T(128)} %bitcast.7, s32[1]{0:T(128)} %bitcast.7), dimensions={0} | concatenate | bytes 96 | tf_op jit(solution)/shard_map/concatenate | solution.py:119
  60.9 7.6 %concatenate.46 = s32[12]{0:T(128)S(1)} concatenate(s32[1]{0:T(128)} %bitcast.2, s32[1]{0:T(128)} %bitcast.3, s32[1]{0:T(128)} %bitcast.2, s32[1]{0:T(128)} %bitcast.3, s32[1]{0:T(128)} %bitcast.4, s32[1]{0:T(128)} %bitcast.5, s32[1]{0:T(128)} %bitcast.4, s32[1]{0:T(128)} %bitcast.5, s32[1]{0:T(128)} %bitcast.6, s32[1]{0:T(128)} %bitcast.7, s32[1]{0:T(128)} %bitcast.6, s32[1]{0:T(128)} %bitcast.7), dimensions={0} | concatenate | bytes 96 | tf_op jit(solution)/shard_map/concatenate | solution.py:120
  68.5 0.1 copy.26
  68.6 0.1 copy.25
  68.7 0.1 copy.24
  68.8 0.8 copy.23
  69.6 0.2 copy.28
  69.8 0.3 copy.44
  70.2 0.2 copy.27
  70.4 0.3 copy.45
  70.7 2.5 %concatenate.58 = f32[12,32768]{1,0:T(8,128)S(1)} concatenate(f32[1,32768]{1,0:T(1,128)} %bitcast.130, f32[1,32768]{1,0:T(1,128)S(1)} %bitcast.129, f32[1,32768]{1,0:T(1,128)S(1)} %bitcast.128, f32[1,32768]{1,0:T(1,128)S(1)} %bitcast.127, f32[4,32768]{1,0:T(4,128)S(1)} %bitcast.123, f32[4,32768]{1,0:T(4,128)S(1)} %bitcast.122), dimensions={0} | concatenate | bytes 3145728 | tf_op jit(solution)/shard_map/concatenate | solution.py:118
  73.3 0.4 copy.37
  73.7 0.1 slice.149
  73.8 2.0 %fusion.10 = f32[4,2,2,128,128]{4,0,3,2,1:T(4,128)S(1)} fusion(f32[2,128,128,12]{2,1,0,3:T(8,128)S(1)} %bitcast.119, s32[12]{0:T(128)S(1)} %concatenate.46, s32[4,2]{0,1:T(2,128)S(1)} %bitcast.137, s32[12]{0:T(128)S(1)} %concatenate.45, s32[4]{0:T(128)S(1)} %slice_reduce_fusion), kind=kOutput, calls=%fused_computation.18 | convolution fusion | flops 37749024 | bytes 2621584 | tf_op jit(solution)/shard_map/dot_general | solution.py:125
  75.8 1.1 copy.30
  76.9 0.0 reduce-scatter.4.cloned.1.call-update
  76.9 28.3 %reduce-scatter.4.cloned.1.call-done = f32[1,2,2,128,128]{4,3,2,1,0:T(8,128)} async-done(((f32[4,2,2,128,128]{4,3,2,1,0:T(8,128)}), f32[1,2,2,128,128]{4,3,2,1,0:T(8,128)}) %reduce-scatter.4.cloned.1.call-update) | async-done | bytes 262160
  (30 shorter events, 0.4 us)
Async XLA Ops:
  6.5 98.7 %reduce-scatter.4.cloned.1.call-start = ((), (), s32[]{:S(2)}) async-start(), calls=%async_computation.1 | async-start | bytes 1310720
  18.1 14.9 %collective-permute-start = (s32[1,10]{1,0:T(1,128)S(1)}, s32[1,10]{1,0:T(1,128)S(1)}, u32[]{:S(2)}, u32[]{:S(2)}) collective-permute-start(s32[1,10]{1,0:T(1,128)S(1)} %pad_add_fusion), channel_id=1, source_target_pairs={{0,1},{1,2},{2,3},{3,4},{4,5},{5,6},{6,7},{7,0},{8,9},{9,10},{10,1... | collective-permute-start | bytes 128 | tf_op jit(solution)/shard_map/ppermute | solution.py:14
  18.1 17.4 %collective-permute-start.1 = (s32[1,10]{1,0:T(1,128)S(1)}, s32[1,10]{1,0:T(1,128)S(1)}, u32[]{:S(2)}, u32[]{:S(2)}) collective-permute-start(s32[1,10]{1,0:T(1,128)S(1)} %pad_add_fusion), channel_id=1, source_target_pairs={{1,0},{2,1},{3,2},{4,3},{5,4},{6,5},{7,6},{0,7},{9,8},{10,9},{11,1... | collective-permute-start | bytes 128 | tf_op jit(solution)/shard_map/ppermute | solution.py:16
  22.0 16.4 %copy-start.3 = (s32[1,1,2]{2,1,0:T(1,128)S(1)}, s32[1,1,2]{2,1,0:T(1,128)}, u32[]{:S(2)}) copy-start(s32[1,1,2]{2,1,0:T(1,128)} %param.11) | copy-start | bytes 28
  35.4 9.1 %collective-permute-start.2 = (bf16[4,2,128,128]{3,2,1,0:T(8,128)(2,1)S(1)}, bf16[4,2,128,128]{3,2,1,0:T(8,128)(2,1)S(1)}, u32[]{:S(2)}, u32[]{:S(2)}) collective-permute-start(bf16[4,2,128,128]{3,2,1,0:T(8,128)(2,1)S(1)} %bitcast.131), channel_id=1, source_target_pairs={{1,0},{2,1},{3,2},{4,3},{5,4},{6,5},{7,6},{0,7},{9,8},{10,9},{11,1... | collective-permute-start | bytes 786440 | tf_op jit(solution)/shard_map/ppermute | solution.py:26
  37.8 7.6 %collective-permute-start.3 = (bf16[4,2,128,128]{3,2,1,0:T(8,128)(2,1)S(1)}, bf16[4,2,128,128]{3,2,1,0:T(8,128)(2,1)S(1)}, u32[]{:S(2)}, u32[]{:S(2)}) collective-permute-start(bf16[4,2,128,128]{3,2,1,0:T(8,128)(2,1)S(1)} %bitcast.132), channel_id=1, source_target_pairs={{7,0},{0,1},{1,2},{2,3},{3,4},{4,5},{5,6},{6,7},{15,8},{8,9},{9,10... | collective-permute-start | bytes 786440 | tf_op jit(solution)/shard_map/ppermute | solution.py:26
  43.7 1.9 %copy-start = (bf16[1,1,4096,256]{3,2,1,0:T(8,128)(2,1)S(1)}, bf16[1,1,4096,256]{3,2,1,0:T(8,128)(2,1)}, u32[]{:S(2)}) copy-start(bf16[1,1,4096,256]{3,2,1,0:T(8,128)(2,1)} %param.7) | copy-start | bytes 6291460
  46.9 1.1 copy-start.1
  46.9 1.1 copy-start.2
  50.4 19.2 %collective-permute-start.5 = (f32[4,2,128,128]{2,3,1,0:T(8,128)S(1)}, f32[4,2,128,128]{2,3,1,0:T(8,128)S(1)}, u32[]{:S(2)}, u32[]{:S(2)}) collective-permute-start(f32[4,2,128,128]{2,3,1,0:T(8,128)S(1)} %pad_maximum_fusion), channel_id=1, source_target_pairs={{1,0},{2,1},{3,2},{4,3},{5,4},{6,5},{7,6},{0,7},{9,8},{10,9},{11,1... | collective-permute-start | bytes 1572872 | tf_op jit(solution)/shard_map/ppermute | solution.py:26
  53.2 16.9 %collective-permute-start.4 = (f32[4,2,128,128]{2,3,1,0:T(8,128)S(1)}, f32[4,2,128,128]{2,3,1,0:T(8,128)S(1)}, u32[]{:S(2)}, u32[]{:S(2)}) collective-permute-start(f32[4,2,128,128]{2,3,1,0:T(8,128)S(1)} %pad_maximum_fusion), channel_id=1, source_target_pairs={{7,0},{0,1},{1,2},{2,3},{3,4},{4,5},{5,6},{6,7},{15,8},{8,9},{9,10... | collective-permute-start | bytes 1572872 | tf_op jit(solution)/shard_map/ppermute | solution.py:26
Sparse Core Ops, SparseCore 0:
  77.0 28.1 reduce-scatter.3
where the time goes:
time: 113 us; the launch traced here: 112 us
  waiting for transfers between devices  29.3 us (26%)
  local copies, waits for them, and re-layouts  27.8 us (25%)
  blocking collectives  20.3 us (18%)
  between operations  14.5 us (13%)
  other arithmetic  7.52 us (7%)
  starting transfers between devices  6.92 us (6%)
  matrix products  5.67 us (5%)
    unnamed x2, waiting for transfers between devices  28.4 us
    all_gather x1, blocking collectives, on_device(): lax.all_gather(density, 'row', axis=1, tiled=True)  10.7 us
    all_gather x1, blocking collectives, on_device(): lax.all_gather(tile_lists, 'row', axis=1, tiled=True)  9.52 us
    concatenate x1, local copies, waits for them, and re-layouts, on_device(): entry_cols = jnp.concatenate([own_cols, lower_cols, upper_cols], 0)  7.6 us
    concatenate x1, local copies, waits for them, and re-layouts, on_device(): entry_rows = jnp.concatenate([own_rows, lower_rows, upper_rows], 0)  7.6 us
    unnamed x16, local copies, waits for them, and re-layouts  4.24 us
    another operation x3, other arithmetic, pair_ids(): pair_rows = jnp.stack([head, head, tail, tail], -1)  3.98 us
    ppermute x1, starting transfers between devices, padded(): lax.ppermute(head, axis, [((i + 1) % count, i) for i in range(count)])  3.54 us
  transfers between devices with their start and end apart: 7, of which 2 were waited for; matrix products, arithmetic and copies ran while one was open for 25% of the time, Pallas kernels for 0%

commit v1 on v0

v1 whole, which is shorter than its diff:
```python
import functools

import jax
import jax.numpy as jnp
from jax import lax
from jax.experimental import pallas as pl
from jax.experimental.pallas import tpu as pltpu
from jax.sharding import PartitionSpec as P

DIGIT = 256
ID_ROWS = 16


def row_route(count, step):
    if count & (count - 1) == 0:
        return [(i, i ^ step) for i in range(count)]
    return [(i, (i + step) % count) for i in range(count)]


def from_peer(block, step):
    return lax.ppermute(block, "row", row_route(lax.axis_size("row"), step))


def to_peer(block, step):
    route = row_route(lax.axis_size("row"), step)
    return lax.ppermute(block, "row", [(target, source) for source, target in route])


def passed_along(block, distance):
    count = lax.axis_size("col")
    return lax.ppermute(block, "col", [((i - distance) % count, i) for i in range(count)])


VMEM = pl.BlockSpec(memory_space=pltpu.VMEM)
SMEM = pl.BlockSpec(memory_space=pltpu.SMEM)


def pack_body(lists, batch, tiles, message, wanted):
    size = tiles.shape[0]
    message[:size, :] = tiles[...]
    row = lax.broadcasted_iota(jnp.int32, (ID_ROWS, tiles.shape[1]), 0)
    digits = jnp.zeros(row.shape, jnp.int32)
    for place in (0, 1):
        tile = lists[place]
        digits = jnp.where(row == 2 * place, tile % DIGIT, digits)
        digits = jnp.where(row == 2 * place + 1, tile // DIGIT, digits)
    message[size:, :] = digits.astype(jnp.float32).astype(message.dtype)
    slot = lax.broadcasted_iota(jnp.int32, wanted.shape, 0)
    wanted[...] = jnp.where(slot == 0, batch[0], batch[1])


def values_body(live, values, weights, kernel, turned, factor):
    points = values.shape[0]
    step = 512
    for start in range(0, points, step):
        turned[:, start : start + step] = values[start : start + step, :].T
    point = lax.broadcasted_iota(jnp.int32, weights.shape, 1)
    factor[...] = jnp.where(point < live[0, 0], weights[...] * kernel[...], 0.0)


def row_ids(message, size):
    digits = message[size:, :].astype(jnp.float32).astype(jnp.int32)
    head = digits[0:1] + DIGIT * digits[1:2]
    tail = digits[2:3] + DIGIT * digits[3:4]
    return head, tail


def route_body(*refs, rows):
    messages = refs[:rows]
    own, lower, upper = refs[rows : rows + 3]
    first, second, for_lower, for_upper = refs[rows + 3 :]
    width = messages[0].shape[1]
    size = 4 * width
    ids = [row_ids(m, size) for m in messages]

    def pick(mask_of, offset):
        total = jnp.zeros((width, width), jnp.bfloat16)
        for m, (head, tail) in zip(messages, ids):
            mask = mask_of(head, tail)
            tile = m[offset : offset + width, :]
            total = jnp.where(mask, tile, total)
        return total

    for pert in (0, 1):
        diag = pert * width
        cross = (2 + pert) * width
        s0, s1 = own[0:1, :], own[1:2, :]
        rows_at = slice(pert * width, (pert + 1) * width)
        first[rows_at, :width] = pick(lambda h, t: h == s0, diag)
        first[rows_at, width:] = pick(lambda h, t: (h == s0) & (t == s1), cross)
        for ref, want in ((second, own), (for_lower, lower), (for_upper, upper)):
            w0, w1 = want[0:1, :], want[1:2, :]
            ref[rows_at, :width] = pick(lambda h, t: (h == w1) & (t == w0), cross)
            ref[rows_at, width:] = pick(lambda h, t: h == w1, diag)


def quadratic(matrix, turned, chunk, rows):
    width = matrix.shape[0] // 2
    product = jnp.dot(matrix, turned[:, chunk], preferred_element_type=jnp.float32)
    side = turned[rows, chunk].astype(jnp.float32)
    return [
        jnp.sum(product[p * width : (p + 1) * width] * side, axis=0, keepdims=True) for p in (0, 1)
    ]


STEP = 512


def begin_body(first, turned, early):
    width = first.shape[0] // 2
    matrix = first[...]
    for start in range(0, turned.shape[1], STEP):
        chunk = slice(start, start + STEP)
        sums = quadratic(matrix, turned, chunk, slice(0, width))
        for p in (0, 1):
            early[p : p + 1, chunk] = sums[p]


def main_body(second, lower, upper, turned, values, early, factor, part, message, scaled):
    width = second.shape[0] // 2
    matrix = second[...] + lower[...] + upper[...]
    total = jnp.zeros(part.shape, jnp.float32)
    for start in range(0, turned.shape[1], STEP):
        chunk = slice(start, start + STEP)
        sums = quadratic(matrix, turned, chunk, slice(width, 2 * width))
        side = turned[:, chunk].astype(jnp.float32)
        lhs = []
        for p in (0, 1):
            potential = factor[:, chunk] * (early[p : p + 1, chunk] + sums[p])
            block = (potential * side).astype(jnp.bfloat16)
            scaled[p * width : (p + 1) * width, chunk] = block[:width]
            lhs.append(block[width:])
        total += jnp.dot(
            jnp.concatenate(lhs, 0), values[chunk, :], preferred_element_type=jnp.float32
        )
    part[...] = total
    message[...] = total.astype(jnp.bfloat16)


def rest_body(scaled, values, part):
    part[...] = jnp.dot(scaled[...], values[...], preferred_element_type=jnp.float32)


def collect_body(*refs, rows):
    messages = refs[:rows]
    own, lower, upper, first, second, from_lower, from_upper = refs[rows : rows + 7]
    outs = refs[rows + 7 :]
    width = messages[0].shape[1]
    size = 4 * width
    w = [(ref[0:1, :], ref[1:2, :]) for ref in (own, lower, upper)]
    for message, out in zip(messages, outs):
        head, tail = row_ids(message, size)
        is_first = head == w[0][0]
        for p in (0, 1):
            at = slice(p * width, (p + 1) * width)
            diag = jnp.where(is_first, first[at, :width], 0.0)
            cross = jnp.where(is_first & (tail == w[0][1]), first[at, width:], 0.0)
            for (s0, s1), ref in zip(w, (second, from_lower, from_upper)):
                block = ref[at, :].astype(jnp.float32)
                diag += jnp.where(head == s1, block[:, width:], 0.0)
                cross += jnp.where((head == s1) & (tail == s0), block[:, :width], 0.0)
            out[p * width : (p + 1) * width, :] = diag.astype(out.dtype)
            out[(2 + p) * width : (3 + p) * width, :] = cross.astype(out.dtype)


def sum_body(*refs):
    total = refs[0][...]
    for ref in refs[1:-1]:
        total += ref[...].astype(jnp.float32)
    refs[-1][...] = total


def on_device(basis_values, weights, kernel, live_points, batch_tiles, density, tile_lists):
    rows = lax.axis_size("row")
    width = density.shape[-1]
    points, basis = basis_values.shape[2:]
    f32, bf16 = jnp.float32, jnp.bfloat16
    shape = jax.ShapeDtypeStruct
    vmem = pltpu.VMEM
    size = 4 * width
    tiles = density.reshape(size, width)
    values = basis_values.reshape(points, basis)
    flops = 2 * points * basis * basis

    message, wanted = pl.pallas_call(
        pack_body,
        in_specs=[SMEM, SMEM, VMEM],
        out_specs=[VMEM, VMEM],
        out_shape=[shape((size + ID_ROWS, width), bf16), shape((8, width), jnp.int32)],
        name="pack",
    )(tile_lists.reshape(-1), batch_tiles.reshape(-1), tiles)
    messages = [message] + [from_peer(message, step) for step in range(1, rows)]
    want_lower = passed_along(wanted, 1)
    want_upper = passed_along(wanted, -1)
    wants = [wanted, want_lower, want_upper]

    turned, factor = pl.pallas_call(
        values_body,
        in_specs=[SMEM, VMEM, VMEM, VMEM],
        out_specs=[VMEM, VMEM],
        out_shape=[shape((basis, points), bf16), shape((1, points), f32)],
        name="turn",
        cost_estimate=pl.CostEstimate(flops=flops, bytes_accessed=0, transcendentals=0),
    )(live_points, values, weights.reshape(1, points), kernel.reshape(1, points))

    square = shape((2 * width, basis), bf16)
    first, second, for_lower, for_upper = pl.pallas_call(
        functools.partial(route_body, rows=rows),
        out_shape=[square] * 4,
        name="route",
    )(*messages, *wants)
    from_upper = passed_along(for_lower, -1)
    from_lower = passed_along(for_upper, 1)

    early = pl.pallas_call(
        begin_body,
        out_shape=shape((2, points), f32),
        name="begin",
        cost_estimate=pl.CostEstimate(flops=flops, bytes_accessed=0, transcendentals=0),
    )(first, turned)

    part_second, send, scaled = pl.pallas_call(
        main_body,
        out_shape=[
            shape((2 * width, basis), f32),
            square,
            shape((2 * width, points), bf16),
        ],
        name="main",
        cost_estimate=pl.CostEstimate(flops=2 * flops, bytes_accessed=0, transcendentals=0),
    )(second, from_lower, from_upper, turned, values, early, factor)
    sums_lower = passed_along(send, 1)
    sums_upper = passed_along(send, -1)

    part_first = pl.pallas_call(
        rest_body,
        out_shape=shape((2 * width, basis), f32),
        name="rest",
        cost_estimate=pl.CostEstimate(flops=flops, bytes_accessed=0, transcendentals=0),
    )(scaled, values)

    outs = pl.pallas_call(
        functools.partial(collect_body, rows=rows),
        out_shape=[shape((size, width), f32)] + [shape((size, width), bf16)] * (rows - 1),
        name="collect",
    )(*messages, *wants, part_first, part_second, sums_lower, sums_upper)
    received = [to_peer(outs[step], step) for step in range(1, rows)]
    owned = pl.pallas_call(sum_body, out_shape=shape((size, width), f32), name="add")(
        outs[0], *received
    )
    return owned.reshape(density.shape)


def solution(mesh):
    placed = (
        P("col", "row", None, None),
        P("col", "row", None),
        P("col", "row", None),
        P("col", "row"),
        P("col", "row", None),
        P("col", "row", None, None, None, None),
        P("col", "row", None),
    )
    return jax.shard_map(
        on_device,
        mesh=mesh,
        in_specs=placed,
        out_specs=P("col", "row", None, None, None, None),
        check_vma=False,
    )
```

time: 113 us -> 55.8 us (0.49)
  local copies, waits for them, and re-layouts: 27.8 us -> 3.36 us
  Pallas kernels: 0 us -> 23.9 us
  blocking collectives: 20.3 us -> 0 us
  waiting for transfers between devices: 29.3 us -> 12.9 us
  between operations: 14.5 us -> 0.72 us
  starting transfers between devices: 6.92 us -> 14.7 us
  other arithmetic: 7.52 us -> 0 us
  matrix products: 5.67 us -> 0 us
    unnamed x2 -> x0, waiting for transfers between devices: 28.4 us -> none
    pallas_call x0 -> x8, Pallas kernels: none -> 23.9 us  [the longest x1 5.76 us: on_device(): pl.pallas_call(main_body, out_shape=[shape((2 * width, basis), f32), squa...]
    all_gather x2 -> x0, blocking collectives: 20.3 us -> none  [the longest x1 10.7 us: on_device(): lax.all_gather(density, 'row', axis=1, tiled=True)]
    concatenate x3 -> x0, local copies, waits for them, and re-layouts: 17.8 us -> none  [the longest x1 7.6 us: on_device(): entry_cols = jnp.concatenate([own_cols, lower_cols, upper_cols], 0)]
    ppermute x6 -> x12, waiting for transfers between devices: 0.99 us -> 12.9 us  [the longest x6 7.31 us: passed_along(): lax.ppermute(block, 'col', [((i - distance) % count, i) for i in range(co...]
    ppermute x6 -> x12, starting transfers between devices: 6.92 us -> 14.7 us  [the longest x6 6.73 us: passed_along(): lax.ppermute(block, 'col', [((i - distance) % count, i) for i in range(co...]
    dot_general x6 -> x0, matrix products: 5.67 us -> none  [the longest x1 2.01 us: on_device(): jnp.dot(matched, entries.reshape(entries.shape[0], -1), precision=lax.Pre...]
    another operation x8 -> x0, other arithmetic: 4.1 us -> none  [the longest x3 3.98 us: pair_ids(): pair_rows = jnp.stack([head, head, tail, tail], -1)]
  transfers between devices with their start and end apart: 7 -> 12, of which waited for: 2 -> 6; matrix products, arithmetic and copies ran while one was open for 25% -> 0% of each run, Pallas kernels for 0% -> 18%
where the time goes in v1:
time: 55.8 us; the launch traced here: 55.6 us
  Pallas kernels  23.9 us (43%)
  starting transfers between devices  14.7 us (26%)
  waiting for transfers between devices  12.9 us (23%)
  local copies, waits for them, and re-layouts  3.36 us (6%)
  between operations  0.72 us (1%)
    ppermute x6, waiting for transfers between devices, passed_along(): lax.ppermute(block, 'col', [((i - distance) % count, i) for i in range(co...  7.31 us
    ppermute x6, starting transfers between devices, passed_along(): lax.ppermute(block, 'col', [((i - distance) % count, i) for i in range(co...  6.73 us
    pallas_call x1, Pallas kernels, on_device(): pl.pallas_call(main_body, out_shape=[shape((2 * width, basis), f32), squa...  5.76 us
    ppermute x3, waiting for transfers between devices, to_peer(): lax.ppermute(block, 'row', [(target, source) for source, target in route])  5.59 us
    ppermute x3, starting transfers between devices, from_peer(): return lax.ppermute(block, 'row', row_route(lax.axis_size('row'), step))  4.49 us
    pallas_call x1, Pallas kernels, on_device(): pl.pallas_call(rest_body, out_shape=shape((2 * width, basis), f32), name=...  3.62 us
    pallas_call x1, Pallas kernels, on_device(): pl.pallas_call(values_body, in_specs=[SMEM, VMEM, VMEM, VMEM], out_specs=...  3.6 us
    ppermute x3, starting transfers between devices, to_peer(): lax.ppermute(block, 'row', [(target, source) for source, target in route])  3.49 us
  transfers between devices with their start and end apart: 12, of which 6 were waited for; matrix products, arithmetic and copies ran while one was open for 0% of the time, Pallas kernels for 18%

profile of v1, /device:TPU:0, one launch (start us, length us, event | category | flops | bytes accessed | tf_op | source)
XLA Modules:
  0.0 55.6 jit_solution(5962845992535484280)
XLA Ops:
  0.0 1.6 %pack.1 = (bf16[528,128]{1,0:T(8,128)(2,1)}, s32[8,128]{1,0:T(8,128)}) custom-call(s32[2]{0:T(128)} %bitcast.13, s32[2]{0:T(128)} %bitcast.14, bf16[512,128]{1,0:T(8,128)(2,1)} %bitcast.10), custom_call_target="tpu_custom_call" | custom-call | tf_op jit(solution)/shard_map/pack/pallas_call | solution.py:185
  1.6 3.9 %collective-permute-start.2 = (bf16[528,128]{1,0:T(8,128)(2,1)}, bf16[528,128]{1,0:T(8,128)(2,1)S(1)}, u32[]{:S(2)}, u32[]{:S(2)}) collective-permute-start(bf16[528,128]{1,0:T(8,128)(2,1)} %get-tuple-element.20.refs_0_), channel_id=1, source_target_pairs={{0,24},{8,16},{16,8},{24,0},{1,25},{9,17},{17,9},{25,1},{2,26},{10... | collective-permute-start | bytes 405512 | tf_op jit(solution)/shard_map/ppermute | solution.py:21
  5.5 0.5 collective-permute-start.1
  6.0 0.1 collective-permute-start
  6.1 2.7 %collective-permute-start.4 = (s32[8,128]{1,0:T(8,128)}, s32[8,128]{1,0:T(8,128)S(1)}, u32[]{:S(2)}, u32[]{:S(2)}) collective-permute-start(s32[8,128]{1,0:T(8,128)} %get-tuple-element.21.refs_4_), channel_id=1, source_target_pairs={{1,0},{2,1},{3,2},{4,3},{5,4},{6,5},{7,6},{0,7},{9,8},{10,9},{11,1... | collective-permute-start | bytes 12296 | tf_op jit(solution)/shard_map/ppermute | solution.py:31
  8.8 0.0 collective-permute-start.3
  8.8 1.5 %collective-permute-done.4.refs_6_ = s32[8,128]{1,0:T(8,128)S(1)} collective-permute-done((s32[8,128]{1,0:T(8,128)}, s32[8,128]{1,0:T(8,128)S(1)}, u32[]{:S(2)}, u32[]{:S(2)}) %collective-permute-start.4) | collective-permute-done | bytes 4128 | tf_op jit(solution)/shard_map/ppermute | solution.py:31
  10.3 0.0 copy-start.10
  10.3 3.5 %collective-permute-done.3.refs_5_ = s32[8,128]{1,0:T(8,128)S(1)} collective-permute-done((s32[8,128]{1,0:T(8,128)}, s32[8,128]{1,0:T(8,128)S(1)}, u32[]{:S(2)}, u32[]{:S(2)}) %collective-permute-start.3) | collective-permute-done | bytes 4128 | tf_op jit(solution)/shard_map/ppermute | solution.py:31
  13.8 0.0 copy-start.11
  13.8 0.0 collective-permute-done.2.refs_3_
  13.8 0.0 collective-permute-done.1.refs_2_
  13.8 0.0 copy-start.1
  13.8 0.0 collective-permute-done.refs_1_
  13.8 0.0 copy-done.10
  13.8 0.5 copy-done.11
  14.4 0.1 copy-done
  14.5 0.1 copy-done.1
  14.5 0.6 %copy-done.2 = bf16[528,128]{1,0:T(8,128)(2,1)} copy-done((bf16[528,128]{1,0:T(8,128)(2,1)}, bf16[528,128]{1,0:T(8,128)(2,1)S(1)}, u32[]{:S(2)}) %copy-start.2) | copy-done | bytes 135192
  15.2 2.1 %route.1 = (bf16[256,256]{1,0:T(8,128)(2,1)}, bf16[256,256]{1,0:T(8,128)(2,1)}, bf16[256,256]{1,0:T(8,128)(2,1)}, bf16[256,256]{1,0:T(8,128)(2,1)}) custom-call(bf16[528,128]{1,0:T(8,128)(2,1)} %get-tuple-element.20.refs_0_, bf16[528,128]{1,0:T(8,128)(2,1)} %copy-done.2, bf16[528,128]{1,0:T(8,128)(2,1)} %copy-done.1, bf16[528,128]{1,0:T(8,128)(2,1)} %copy-done, ...), custom_call_target="tpu_custom_call" | custom-call | tf_op jit(solution)/shard_map/route/pallas_call | solution.py:207
  17.2 0.0 collective-permute-start.5
  17.2 3.5 %collective-permute-start.6 = (bf16[256,256]{1,0:T(8,128)(2,1)}, bf16[256,256]{1,0:T(8,128)(2,1)S(1)}, u32[]{:S(2)}, u32[]{:S(2)}) collective-permute-start(bf16[256,256]{1,0:T(8,128)(2,1)} %get-tuple-element.24), channel_id=1, source_target_pairs={{1,0},{2,1},{3,2},{4,3},{5,4},{6,5},{7,6},{0,7},{9,8},{10,9},{11,1... | collective-permute-start | bytes 393224 | tf_op jit(solution)/shard_map/ppermute | solution.py:31
  21.4 3.6 %turn.1 = (bf16[256,4096]{1,0:T(8,128)(2,1)}, f32[1,4096]{1,0:T(1,128)}) custom-call(s32[1,1]{1,0:T(1,128)S(6)} %copy.8.live, bf16[4096,256]{1,0:T(8,128)(2,1)} %bitcast.7, f32[1,4096]{1,0:T(1,128)} %bitcast.11, f32[1,4096]{1,0:T(1,128)} %bitcast.12), custom_call_target="tpu_custom_call" | custom-call | flops 536870912 | tf_op jit(solution)/shard_map/turn/pallas_call | solution.py:197
  25.0 3.0 %begin.1.early = f32[2,4096]{1,0:T(2,128)} custom-call(bf16[256,256]{1,0:T(8,128)(2,1)} %get-tuple-element.26.first, bf16[256,4096]{1,0:T(8,128)(2,1)} %get-tuple-element.25.turned), custom_call_target="tpu_custom_call" | custom-call | flops 536870912 | tf_op jit(solution)/shard_map/begin/pallas_call | solution.py:215
  28.1 0.0 collective-permute-done.5.lower
  28.1 0.0 collective-permute-done.6.upper
  28.1 0.0 copy-start.4
  28.1 0.7 %copy-done.3 = bf16[256,256]{1,0:T(8,128)(2,1)} copy-done((bf16[256,256]{1,0:T(8,128)(2,1)}, bf16[256,256]{1,0:T(8,128)(2,1)S(1)}, u32[]{:S(2)}) %copy-start.3) | copy-done | bytes 131096
  28.7 0.0 copy-done.4
  28.8 5.8 %main.1 = (f32[256,256]{1,0:T(8,128)}, bf16[256,256]{1,0:T(8,128)(2,1)}, bf16[256,4096]{1,0:T(8,128)(2,1)}) custom-call(bf16[256,256]{1,0:T(8,128)(2,1)} %get-tuple-element.22.second, bf16[256,256]{1,0:T(8,128)(2,1)} %copy-done.3, bf16[256,256]{1,0:T(8,128)(2,1)} %copy-done.4, bf16[256,4096]{1,0:T(8,128)(2,1)} %get-tuple-element.25.turned, ...), custom_call_target="tpu_custom_call" | custom-call | flops 1073741824 | tf_op jit(solution)/shard_map/main/pallas_call | solution.py:222
  34.5 0.0 collective-permute-start.8
  34.5 0.5 collective-permute-start.7
  35.1 3.6 %rest.1.refs_7_ = f32[256,256]{1,0:T(8,128)} custom-call(bf16[256,4096]{1,0:T(8,128)(2,1)} %get-tuple-element.28.scaled, bf16[4096,256]{1,0:T(8,128)(2,1)} %bitcast.9), custom_call_target="tpu_custom_call" | custom-call | flops 536870912 | tf_op jit(solution)/shard_map/rest/pallas_call | solution.py:235
  38.7 0.0 collective-permute-done.8.refs_10_
  38.7 2.3 %collective-permute-done.7.refs_9_ = bf16[256,256]{1,0:T(8,128)(2,1)S(1)} collective-permute-done((bf16[256,256]{1,0:T(8,128)(2,1)}, bf16[256,256]{1,0:T(8,128)(2,1)S(1)}, u32[]{:S(2)}, u32[]{:S(2)}) %collective-permute-start.7) | collective-permute-done | bytes 131104 | tf_op jit(solution)/shard_map/ppermute | solution.py:31
  40.9 0.0 copy-done.8
  41.0 0.6 %copy-done.9 = bf16[256,256]{1,0:T(8,128)(2,1)} copy-done((bf16[256,256]{1,0:T(8,128)(2,1)}, bf16[256,256]{1,0:T(8,128)(2,1)S(1)}, u32[]{:S(2)}) %copy-start.9) | copy-done | bytes 131096
  41.6 2.4 %collect.1 = (f32[512,128]{1,0:T(8,128)}, bf16[512,128]{1,0:T(8,128)(2,1)}, bf16[512,128]{1,0:T(8,128)(2,1)}, bf16[512,128]{1,0:T(8,128)(2,1)}) custom-call(bf16[528,128]{1,0:T(8,128)(2,1)} %get-tuple-element.20.refs_0_, bf16[528,128]{1,0:T(8,128)(2,1)} %copy-done.2, bf16[528,128]{1,0:T(8,128)(2,1)} %copy-done.1, bf16[528,128]{1,0:T(8,128)(2,1)} %copy-done, ...), custom_call_target="tpu_custom_call" | custom-call | tf_op jit(solution)/shard_map/collect/pallas_call | solution.py:242
  44.0 1.5 %collective-permute-start.9 = (bf16[512,128]{1,0:T(8,128)(2,1)}, bf16[512,128]{1,0:T(8,128)(2,1)S(1)}, u32[]{:S(2)}, u32[]{:S(2)}) collective-permute-start(bf16[512,128]{1,0:T(8,128)(2,1)} %get-tuple-element.32), channel_id=1, source_target_pairs={{8,0},{0,8},{24,16},{16,24},{9,1},{1,9},{25,17},{17,25},{10,2},{2,... | collective-permute-start | bytes 393224 | tf_op jit(solution)/shard_map/ppermute | solution.py:26
  45.4 1.5 %collective-permute-start.10 = (bf16[512,128]{1,0:T(8,128)(2,1)}, bf16[512,128]{1,0:T(8,128)(2,1)S(1)}, u32[]{:S(2)}, u32[]{:S(2)}) collective-permute-start(bf16[512,128]{1,0:T(8,128)(2,1)} %get-tuple-element.33), channel_id=1, source_target_pairs={{16,0},{24,8},{0,16},{8,24},{17,1},{25,9},{1,17},{9,25},{18,2},{26... | collective-permute-start | bytes 393224 | tf_op jit(solution)/shard_map/ppermute | solution.py:26
  47.0 0.5 collective-permute-start.11
  47.4 2.3 %collective-permute-done.9.refs_1_ = bf16[512,128]{1,0:T(8,128)(2,1)S(1)} collective-permute-done((bf16[512,128]{1,0:T(8,128)(2,1)}, bf16[512,128]{1,0:T(8,128)(2,1)S(1)}, u32[]{:S(2)}, u32[]{:S(2)}) %collective-permute-start.9) | collective-permute-done | bytes 131104 | tf_op jit(solution)/shard_map/ppermute | solution.py:26
  49.8 1.2 %collective-permute-done.10.refs_2_ = bf16[512,128]{1,0:T(8,128)(2,1)S(1)} collective-permute-done((bf16[512,128]{1,0:T(8,128)(2,1)}, bf16[512,128]{1,0:T(8,128)(2,1)S(1)}, u32[]{:S(2)}, u32[]{:S(2)}) %collective-permute-start.10) | collective-permute-done | bytes 131104 | tf_op jit(solution)/shard_map/ppermute | solution.py:26
  51.0 2.1 %collective-permute-done.11.refs_3_ = bf16[512,128]{1,0:T(8,128)(2,1)S(1)} collective-permute-done((bf16[512,128]{1,0:T(8,128)(2,1)}, bf16[512,128]{1,0:T(8,128)(2,1)S(1)}, u32[]{:S(2)}, u32[]{:S(2)}) %collective-permute-start.11) | collective-permute-done | bytes 131104 | tf_op jit(solution)/shard_map/ppermute | solution.py:26
  53.0 0.0 copy-done.5
  53.1 0.0 copy-done.6
  53.1 0.6 %copy-done.7 = bf16[512,128]{1,0:T(8,128)(2,1)} copy-done((bf16[512,128]{1,0:T(8,128)(2,1)}, bf16[512,128]{1,0:T(8,128)(2,1)S(1)}, u32[]{:S(2)}) %copy-start.7) | copy-done | bytes 131096
  53.7 1.9 %add.1 = f32[512,128]{1,0:T(8,128)} custom-call(f32[512,128]{1,0:T(8,128)} %get-tuple-element.31.refs_0_, bf16[512,128]{1,0:T(8,128)(2,1)} %copy-done.5, bf16[512,128]{1,0:T(8,128)(2,1)} %copy-done.6, bf16[512,128]{1,0:T(8,128)(2,1)} %copy-done.7), custom_call_target="tpu_custom_call" | custom-call | tf_op jit(solution)/shard_map/add/pallas_call | solution.py:248
  (8 shorter events, 0.0 us)
Async XLA Ops:
  1.6 12.2 %collective-permute-start.2 = (bf16[528,128]{1,0:T(8,128)(2,1)}, bf16[528,128]{1,0:T(8,128)(2,1)S(1)}, u32[]{:S(2)}, u32[]{:S(2)}) collective-permute-start(bf16[528,128]{1,0:T(8,128)(2,1)} %get-tuple-element.20.refs_0_), channel_id=1, source_target_pairs={{0,24},{8,16},{16,8},{24,0},{1,25},{9,17},{17,9},{25,1},{2,26},{10... | collective-permute-start | bytes 405512 | tf_op jit(solution)/shard_map/ppermute | solution.py:21
  5.5 8.3 %collective-permute-start.1 = (bf16[528,128]{1,0:T(8,128)(2,1)}, bf16[528,128]{1,0:T(8,128)(2,1)S(1)}, u32[]{:S(2)}, u32[]{:S(2)}) collective-permute-start(bf16[528,128]{1,0:T(8,128)(2,1)} %get-tuple-element.20.refs_0_), channel_id=1, source_target_pairs={{0,16},{8,24},{16,0},{24,8},{1,17},{9,25},{17,1},{25,9},{2,18},{10... | collective-permute-start | bytes 405512 | tf_op jit(solution)/shard_map/ppermute | solution.py:21
  6.0 7.8 %collective-permute-start = (bf16[528,128]{1,0:T(8,128)(2,1)}, bf16[528,128]{1,0:T(8,128)(2,1)S(1)}, u32[]{:S(2)}, u32[]{:S(2)}) collective-permute-start(bf16[528,128]{1,0:T(8,128)(2,1)} %get-tuple-element.20.refs_0_), channel_id=1, source_target_pairs={{0,8},{8,0},{16,24},{24,16},{1,9},{9,1},{17,25},{25,17},{2,10},{10... | collective-permute-start | bytes 405512 | tf_op jit(solution)/shard_map/ppermute | solution.py:21
  6.1 4.2 %collective-permute-start.4 = (s32[8,128]{1,0:T(8,128)}, s32[8,128]{1,0:T(8,128)S(1)}, u32[]{:S(2)}, u32[]{:S(2)}) collective-permute-start(s32[8,128]{1,0:T(8,128)} %get-tuple-element.21.refs_4_), channel_id=1, source_target_pairs={{1,0},{2,1},{3,2},{4,3},{5,4},{6,5},{7,6},{0,7},{9,8},{10,9},{11,1... | collective-permute-start | bytes 12296 | tf_op jit(solution)/shard_map/ppermute | solution.py:31
  8.8 5.0 %collective-permute-start.3 = (s32[8,128]{1,0:T(8,128)}, s32[8,128]{1,0:T(8,128)S(1)}, u32[]{:S(2)}, u32[]{:S(2)}) collective-permute-start(s32[8,128]{1,0:T(8,128)} %get-tuple-element.21.refs_4_), channel_id=1, source_target_pairs={{7,0},{0,1},{1,2},{2,3},{3,4},{4,5},{5,6},{6,7},{15,8},{8,9},{9,10... | collective-permute-start | bytes 12296 | tf_op jit(solution)/shard_map/ppermute | solution.py:31
  10.3 3.5 %copy-start.10 = (s32[8,128]{1,0:T(8,128)}, s32[8,128]{1,0:T(8,128)S(1)}, u32[]{:S(2)}) copy-start(s32[8,128]{1,0:T(8,128)S(1)} %collective-permute-done.4.refs_6_) | copy-start | bytes 12292
  13.8 0.6 %copy-start.11 = (s32[8,128]{1,0:T(8,128)}, s32[8,128]{1,0:T(8,128)S(1)}, u32[]{:S(2)}) copy-start(s32[8,128]{1,0:T(8,128)S(1)} %collective-permute-done.3.refs_5_) | copy-start | bytes 12292
  13.8 0.7 %copy-start = (bf16[528,128]{1,0:T(8,128)(2,1)}, bf16[528,128]{1,0:T(8,128)(2,1)S(1)}, u32[]{:S(2)}) copy-start(bf16[528,128]{1,0:T(8,128)(2,1)S(1)} %collective-permute-done.2.refs_3_) | copy-start | bytes 405508
  13.8 0.7 %copy-start.1 = (bf16[528,128]{1,0:T(8,128)(2,1)}, bf16[528,128]{1,0:T(8,128)(2,1)S(1)}, u32[]{:S(2)}) copy-start(bf16[528,128]{1,0:T(8,128)(2,1)S(1)} %collective-permute-done.1.refs_2_) | copy-start | bytes 405508
  14.5 0.6 %copy-start.2 = (bf16[528,128]{1,0:T(8,128)(2,1)}, bf16[528,128]{1,0:T(8,128)(2,1)S(1)}, u32[]{:S(2)}) copy-start(bf16[528,128]{1,0:T(8,128)(2,1)S(1)} %collective-permute-done.refs_1_) | copy-start | bytes 405508
  17.2 10.8 %collective-permute-start.5 = (bf16[256,256]{1,0:T(8,128)(2,1)}, bf16[256,256]{1,0:T(8,128)(2,1)S(1)}, u32[]{:S(2)}, u32[]{:S(2)}) collective-permute-start(bf16[256,256]{1,0:T(8,128)(2,1)} %get-tuple-element.23), channel_id=1, source_target_pairs={{7,0},{0,1},{1,2},{2,3},{3,4},{4,5},{5,6},{6,7},{15,8},{8,9},{9,10... | collective-permute-start | bytes 393224 | tf_op jit(solution)/shard_map/ppermute | solution.py:31
  17.2 10.8 %collective-permute-start.6 = (bf16[256,256]{1,0:T(8,128)(2,1)}, bf16[256,256]{1,0:T(8,128)(2,1)S(1)}, u32[]{:S(2)}, u32[]{:S(2)}) collective-permute-start(bf16[256,256]{1,0:T(8,128)(2,1)} %get-tuple-element.24), channel_id=1, source_target_pairs={{1,0},{2,1},{3,2},{4,3},{5,4},{6,5},{7,6},{0,7},{9,8},{10,9},{11,1... | collective-permute-start | bytes 393224 | tf_op jit(solution)/shard_map/ppermute | solution.py:31
  28.1 0.7 %copy-start.3 = (bf16[256,256]{1,0:T(8,128)(2,1)}, bf16[256,256]{1,0:T(8,128)(2,1)S(1)}, u32[]{:S(2)}) copy-start(bf16[256,256]{1,0:T(8,128)(2,1)S(1)} %collective-permute-done.5.lower) | copy-start | bytes 393220
  28.1 0.7 %copy-start.4 = (bf16[256,256]{1,0:T(8,128)(2,1)}, bf16[256,256]{1,0:T(8,128)(2,1)S(1)}, u32[]{:S(2)}) copy-start(bf16[256,256]{1,0:T(8,128)(2,1)S(1)} %collective-permute-done.6.upper) | copy-start | bytes 393220
  34.5 4.1 %collective-permute-start.8 = (bf16[256,256]{1,0:T(8,128)(2,1)}, bf16[256,256]{1,0:T(8,128)(2,1)S(1)}, u32[]{:S(2)}, u32[]{:S(2)}) collective-permute-start(bf16[256,256]{1,0:T(8,128)(2,1)} %get-tuple-element.30), channel_id=1, source_target_pairs={{1,0},{2,1},{3,2},{4,3},{5,4},{6,5},{7,6},{0,7},{9,8},{10,9},{11,1... | collective-permute-start | bytes 393224 | tf_op jit(solution)/shard_map/ppermute | solution.py:31
  34.5 6.4 %collective-permute-start.7 = (bf16[256,256]{1,0:T(8,128)(2,1)}, bf16[256,256]{1,0:T(8,128)(2,1)S(1)}, u32[]{:S(2)}, u32[]{:S(2)}) collective-permute-start(bf16[256,256]{1,0:T(8,128)(2,1)} %get-tuple-element.30), channel_id=1, source_target_pairs={{7,0},{0,1},{1,2},{2,3},{3,4},{4,5},{5,6},{6,7},{15,8},{8,9},{9,10... | collective-permute-start | bytes 393224 | tf_op jit(solution)/shard_map/ppermute | solution.py:31
  38.7 2.3 %copy-start.8 = (bf16[256,256]{1,0:T(8,128)(2,1)}, bf16[256,256]{1,0:T(8,128)(2,1)S(1)}, u32[]{:S(2)}) copy-start(bf16[256,256]{1,0:T(8,128)(2,1)S(1)} %collective-permute-done.8.refs_10_) | copy-start | bytes 393220
  40.9 0.7 %copy-start.9 = (bf16[256,256]{1,0:T(8,128)(2,1)}, bf16[256,256]{1,0:T(8,128)(2,1)S(1)}, u32[]{:S(2)}) copy-start(bf16[256,256]{1,0:T(8,128)(2,1)S(1)} %collective-permute-done.7.refs_9_) | copy-start | bytes 393220
  44.0 5.8 %collective-permute-start.9 = (bf16[512,128]{1,0:T(8,128)(2,1)}, bf16[512,128]{1,0:T(8,128)(2,1)S(1)}, u32[]{:S(2)}, u32[]{:S(2)}) collective-permute-start(bf16[512,128]{1,0:T(8,128)(2,1)} %get-tuple-element.32), channel_id=1, source_target_pairs={{8,0},{0,8},{24,16},{16,24},{9,1},{1,9},{25,17},{17,25},{10,2},{2,... | collective-permute-start | bytes 393224 | tf_op jit(solution)/shard_map/ppermute | solution.py:26
  45.4 5.5 %collective-permute-start.10 = (bf16[512,128]{1,0:T(8,128)(2,1)}, bf16[512,128]{1,0:T(8,128)(2,1)S(1)}, u32[]{:S(2)}, u32[]{:S(2)}) collective-permute-start(bf16[512,128]{1,0:T(8,128)(2,1)} %get-tuple-element.33), channel_id=1, source_target_pairs={{16,0},{24,8},{0,16},{8,24},{17,1},{25,9},{1,17},{9,25},{18,2},{26... | collective-permute-start | bytes 393224 | tf_op jit(solution)/shard_map/ppermute | solution.py:26
  47.0 6.1 %collective-permute-start.11 = (bf16[512,128]{1,0:T(8,128)(2,1)}, bf16[512,128]{1,0:T(8,128)(2,1)S(1)}, u32[]{:S(2)}, u32[]{:S(2)}) collective-permute-start(bf16[512,128]{1,0:T(8,128)(2,1)} %get-tuple-element.34), channel_id=1, source_target_pairs={{24,0},{16,8},{8,16},{0,24},{25,1},{17,9},{9,17},{1,25},{26,2},{18... | collective-permute-start | bytes 393224 | tf_op jit(solution)/shard_map/ppermute | solution.py:26
  49.8 3.3 %copy-start.5 = (bf16[512,128]{1,0:T(8,128)(2,1)}, bf16[512,128]{1,0:T(8,128)(2,1)S(1)}, u32[]{:S(2)}) copy-start(bf16[512,128]{1,0:T(8,128)(2,1)S(1)} %collective-permute-done.9.refs_1_) | copy-start | bytes 393220
  51.0 2.1 %copy-start.6 = (bf16[512,128]{1,0:T(8,128)(2,1)}, bf16[512,128]{1,0:T(8,128)(2,1)S(1)}, u32[]{:S(2)}) copy-start(bf16[512,128]{1,0:T(8,128)(2,1)S(1)} %collective-permute-done.10.refs_2_) | copy-start | bytes 393220
  53.0 0.7 %copy-start.7 = (bf16[512,128]{1,0:T(8,128)(2,1)}, bf16[512,128]{1,0:T(8,128)(2,1)S(1)}, u32[]{:S(2)}) copy-start(bf16[512,128]{1,0:T(8,128)(2,1)S(1)} %collective-permute-done.11.refs_3_) | copy-start | bytes 393220

commit v2 on v1

--- a/solution.py
+++ b/solution.py
@@ -9,6 +9,7 @@
 
 DIGIT = 256
 ID_ROWS = 16
+LIMIT = 16 * 1024 * 1024
 
 
 def row_route(count, step):
@@ -26,18 +27,47 @@
     return lax.ppermute(block, "row", [(target, source) for source, target in route])
 
 
-def passed_along(block, distance):
-    count = lax.axis_size("col")
-    return lax.ppermute(block, "col", [((i - distance) % count, i) for i in range(count)])
-
-
-VMEM = pl.BlockSpec(memory_space=pltpu.VMEM)
-SMEM = pl.BlockSpec(memory_space=pltpu.SMEM)
-
-
-def pack_body(lists, batch, tiles, message, wanted):
+def col_routes(count):
+    if count % 2 == 0:
+        mate = [(i, i ^ 1) for i in range(count)]
+        link = [(i, (i + 1 if i % 2 else i - 1) % count) for i in range(count)]
+        return link, mate
+    return ([(i, (i + step) % count) for i in range(count)] for step in (1, -1))
+
+
+def to_sides(blocks):
+    routes = col_routes(lax.axis_size("col"))
+    return [lax.ppermute(block, "col", route) for block, route in zip(blocks, routes)]
+
+
+def back_to_sides(blocks):
+    routes = col_routes(lax.axis_size("col"))
+    return [
+        lax.ppermute(block, "col", [(target, source) for source, target in route])
+        for block, route in zip(blocks, routes)
+    ]
+
+
+def run(name, body, outs, scalars, arrays, flops=0):
+    return pl.pallas_call(
+        body,
+        in_specs=[pl.BlockSpec(memory_space=pltpu.SMEM)] * len(scalars)
+        + [pl.BlockSpec(memory_space=pltpu.VMEM)] * len(arrays),
+        out_shape=outs,
+        name=name,
+        cost_estimate=pl.CostEstimate(flops=flops, bytes_accessed=0, transcendentals=0),
+        compiler_params=pltpu.CompilerParams(vmem_limit_bytes=LIMIT),
+    )(*scalars, *(pltpu.with_memory_space_constraint(x, pltpu.VMEM) for x in arrays))
+
+
+def in_hbm(x):
+    return pltpu.with_memory_space_constraint(x, pltpu.HBM)
+
+
+def pack_body(lists, batch, tiles, message, wanted, arrived):
     size = tiles.shape[0]
-    message[:size, :] = tiles[...]
+    copy = pltpu.make_async_copy(tiles, message.at[:size, :], arrived)
+    copy.start()
     row = lax.broadcasted_iota(jnp.int32, (ID_ROWS, tiles.shape[1]), 0)
     digits = jnp.zeros(row.shape, jnp.int32)
     for place in (0, 1):
@@ -47,15 +77,30 @@
     message[size:, :] = digits.astype(jnp.float32).astype(message.dtype)
     slot = lax.broadcasted_iota(jnp.int32, wanted.shape, 0)
     wanted[...] = jnp.where(slot == 0, batch[0], batch[1])
-
-
-def values_body(live, values, weights, kernel, turned, factor):
+    copy.wait()
+
+
+def values_body(live, after, values, weights, kernel, turned, kept, factor, other, arrived):
     points = values.shape[0]
     step = 512
-    for start in range(0, points, step):
-        turned[:, start : start + step] = values[start : start + step, :].T
-    point = lax.broadcasted_iota(jnp.int32, weights.shape, 1)
-    factor[...] = jnp.where(point < live[0, 0], weights[...] * kernel[...], 0.0)
+    chunks = [slice(start, start + step) for start in range(0, points, step)]
+    copies = [
+        pltpu.make_async_copy(values.at[chunk, :], kept.at[chunk, :], arrived.at[i])
+        for i, chunk in enumerate(chunks)
+    ]
+    side = [
+        pltpu.make_async_copy(weights, factor, arrived.at[len(chunks)]),
+        pltpu.make_async_copy(kernel, other, arrived.at[len(chunks) + 1]),
+    ]
+    for copy in copies + side:
+        copy.start()
+    for chunk, copy in zip(chunks, copies):
+        copy.wait()
+        turned[:, chunk] = kept[chunk, :].T
+    for copy in side:
+        copy.wait()
+    point = lax.broadcasted_iota(jnp.int32, factor.shape, 1)
+    factor[...] = jnp.where(point < live[0], factor[...] * other[...], 0.0)
 
 
 def row_ids(message, size):
@@ -68,7 +113,7 @@
 def route_body(*refs, rows):
     messages = refs[:rows]
     own, lower, upper = refs[rows : rows + 3]
-    first, second, for_lower, for_upper = refs[rows + 3 :]
+    first, second, for_lower, for_upper = refs[rows + 4 :]
     width = messages[0].shape[1]
     size = 4 * width
     ids = [row_ids(m, size) for m in messages]
@@ -175,78 +220,106 @@
     width = density.shape[-1]
     points, basis = basis_values.shape[2:]
     f32, bf16 = jnp.float32, jnp.bfloat16
-    shape = jax.ShapeDtypeStruct
-    vmem = pltpu.VMEM
     size = 4 * width
-    tiles = density.reshape(size, width)
     values = basis_values.reshape(points, basis)
     flops = 2 * points * basis * basis
 
     message, wanted = pl.pallas_call(
         pack_body,
-        in_specs=[SMEM, SMEM, VMEM],
-        out_specs=[VMEM, VMEM],
-        out_shape=[shape((size + ID_ROWS, width), bf16), shape((8, width), jnp.int32)],
+        in_specs=[
+            pl.BlockSpec(memory_space=pltpu.SMEM),
+            pl.BlockSpec(memory_space=pltpu.SMEM),
+            pl.BlockSpec(memory_space=pltpu.HBM),
+        ],
+        out_shape=[pltpu.VMEM((size + ID_ROWS, width), bf16), pltpu.VMEM((8, width), jnp.int32)],
+        scratch_shapes=[pltpu.SemaphoreType.DMA],
         name="pack",
-    )(tile_lists.reshape(-1), batch_tiles.reshape(-1), tiles)
+        compiler_params=pltpu.CompilerParams(vmem_limit_bytes=LIMIT),
+    )(
+        in_hbm(tile_lists.reshape(-1)),
+        in_hbm(batch_tiles.reshape(-1)),
+        in_hbm(density.reshape(size, width)),
+    )
     messages = [message] + [from_peer(message, step) for step in range(1, rows)]
-    want_lower = passed_along(wanted, 1)
-    want_upper = passed_along(wanted, -1)
-    wants = [wanted, want_lower, want_upper]
-
-    turned, factor = pl.pallas_call(
+    wants = [wanted] + to_sides([wanted, wanted])
+
+    hbm = pl.BlockSpec(memory_space=pltpu.HBM)
+    turned, kept, factor = pl.pallas_call(
         values_body,
-        in_specs=[SMEM, VMEM, VMEM, VMEM],
-        out_specs=[VMEM, VMEM],
-        out_shape=[shape((basis, points), bf16), shape((1, points), f32)],
+        in_specs=[
+            pl.BlockSpec(memory_space=pltpu.SMEM),
+            pl.BlockSpec(memory_space=pltpu.VMEM),
+            hbm,
+            hbm,
+            hbm,
+        ],
+        out_shape=[
+            pltpu.VMEM((basis, points), bf16),
+            pltpu.VMEM((points, basis), bf16),
+            pltpu.VMEM((1, points), f32),
+        ],
+        scratch_shapes=[
+            pltpu.VMEM((1, points), f32),
+            pltpu.SemaphoreType.DMA((points // 512 + 2,)),
+        ],
         name="turn",
         cost_estimate=pl.CostEstimate(flops=flops, bytes_accessed=0, transcendentals=0),
-    )(live_points, values, weights.reshape(1, points), kernel.reshape(1, points))
-
-    square = shape((2 * width, basis), bf16)
-    first, second, for_lower, for_upper = pl.pallas_call(
+        compiler_params=pltpu.CompilerParams(vmem_limit_bytes=LIMIT),
+    )(
+        live_points.reshape(-1),
+        pltpu.with_memory_space_constraint(wanted, pltpu.VMEM),
+        in_hbm(values),
+        in_hbm(weights.reshape(1, points)),
+        in_hbm(kernel.reshape(1, points)),
+    )
+
+    square = pltpu.VMEM((2 * width, basis), bf16)
+    first, second, *answers = run(
+        "route",
         functools.partial(route_body, rows=rows),
-        out_shape=[square] * 4,
-        name="route",
-    )(*messages, *wants)
-    from_upper = passed_along(for_lower, -1)
-    from_lower = passed_along(for_upper, 1)
-
-    early = pl.pallas_call(
-        begin_body,
-        out_shape=shape((2, points), f32),
-        name="begin",
-        cost_estimate=pl.CostEstimate(flops=flops, bytes_accessed=0, transcendentals=0),
-    )(first, turned)
-
-    part_second, send, scaled = pl.pallas_call(
+        [square] * 4,
+        [],
+        messages + wants + [factor],
+    )
+    answers = back_to_sides(answers)
+
+    early = run(
+        "begin", begin_body, pltpu.VMEM((2, points), f32), [], [first, turned], flops
+    )
+
+    part_second, send, scaled = run(
+        "main",
         main_body,
-        out_shape=[
-            shape((2 * width, basis), f32),
+        [
+            pltpu.VMEM((2 * width, basis), f32),
             square,
-            shape((2 * width, points), bf16),
-        ],
-        name="main",
-        cost_estimate=pl.CostEstimate(flops=2 * flops, bytes_accessed=0, transcendentals=0),
-    )(second, from_lower, from_upper, turned, values, early, factor)
-    sums_lower = passed_along(send, 1)
-    sums_upper = passed_along(send, -1)
-
-    part_first = pl.pallas_call(
+            pltpu.VMEM((2 * width, points), bf16),
+        ],
+        [],
+        [second, *answers, turned, kept, early, factor],
+        2 * flops,
+    )
+    sums = to_sides([send, send])
+
+    part_first = run(
+        "rest",
         rest_body,
-        out_shape=shape((2 * width, basis), f32),
-        name="rest",
-        cost_estimate=pl.CostEstimate(flops=flops, bytes_accessed=0, transcendentals=0),
-    )(scaled, values)
-
-    outs = pl.pallas_call(
+        pltpu.VMEM((2 * width, basis), f32),
+        [],
+        [scaled, kept],
+        flops,
+    )
+
+    outs = run(
+        "collect",
         functools.partial(collect_body, rows=rows),
-        out_shape=[shape((size, width), f32)] + [shape((size, width), bf16)] * (rows - 1),
-        name="collect",
-    )(*messages, *wants, part_first, part_second, sums_lower, sums_upper)
+        [pltpu.VMEM((size, width), f32)] + [pltpu.VMEM((size, width), bf16)] * (rows - 1),
+        [],
+        messages + wants + [part_first, part_second] + sums,
+    )
     received = [to_peer(outs[step], step) for step in range(1, rows)]
-    owned = pl.pallas_call(sum_body, out_shape=shape((size, width), f32), name="add")(
-        outs[0], *received
+    owned = run(
+        "add", sum_body, jax.ShapeDtypeStruct((size, width), f32), [], [outs[0]] + received
     )
     return owned.reshape(density.shape)
 

time: 55.8 us -> 39.9 us (0.72)
  Pallas kernels: 23.9 us -> 8.52 us
  local copies, waits for them, and re-layouts: 3.36 us -> 0 us
  starting transfers between devices: 14.7 us -> 16.2 us
  waiting for transfers between devices: 12.9 us -> 14.3 us
    pallas_call x8, Pallas kernels: 23.9 us -> 8.52 us  [the longest x6 4.84 us: run(): pl.pallas_call(body, in_specs=[pl.BlockSpec(memory_space=pltpu.SMEM)] * l...]
    unnamed x24 -> x0, local copies, waits for them, and re-layouts: 3.36 us -> none
    ppermute x6, starting transfers between devices: 6.73 us -> 8.02 us  [the longest x4 5.64 us: to_sides(): lax.ppermute(block, 'col', route)]
    ppermute x6, waiting for transfers between devices: 7.31 us -> 8.26 us  [the longest x4 4.19 us: to_sides(): lax.ppermute(block, 'col', route)]
  transfers between devices with their start and end apart: 12 -> 12, of which waited for: 6 -> 4; matrix products, arithmetic and copies ran while one was open for 0% -> 0% of each run, Pallas kernels for 18% -> 9%
where the time goes in v2:
time: 39.9 us; the launch traced here: 39.7 us
  starting transfers between devices  16.2 us (41%)
  waiting for transfers between devices  14.3 us (36%)
  Pallas kernels  8.52 us (21%)
  between operations  0.76 us (2%)
    ppermute x3, waiting for transfers between devices, to_peer(): lax.ppermute(block, 'row', [(target, source) for source, target in route])  5.99 us
    ppermute x4, starting transfers between devices, to_sides(): lax.ppermute(block, 'col', route)  5.64 us
    pallas_call x6, Pallas kernels, run(): pl.pallas_call(body, in_specs=[pl.BlockSpec(memory_space=pltpu.SMEM)] * l...  4.84 us
    ppermute x3, starting transfers between devices, from_peer(): return lax.ppermute(block, 'row', row_route(lax.axis_size('row'), step))  4.63 us
    ppermute x4, waiting for transfers between devices, to_sides(): lax.ppermute(block, 'col', route)  4.19 us
    ppermute x2, waiting for transfers between devices, back_to_sides(): lax.ppermute(block, 'col', [(target, source) for source, target in route])  4.07 us
    ppermute x3, starting transfers between devices, to_peer(): lax.ppermute(block, 'row', [(target, source) for source, target in route])  3.55 us
    ppermute x2, starting transfers between devices, back_to_sides(): lax.ppermute(block, 'col', [(target, source) for source, target in route])  2.38 us
  transfers between devices with their start and end apart: 12, of which 4 were waited for; matrix products, arithmetic and copies ran while one was open for 0% of the time, Pallas kernels for 9%

profile of v2, /device:TPU:0, one launch (start us, length us, event | category | flops | bytes accessed | tf_op | source)
XLA Modules:
  0.0 39.7 jit_solution(6726798284568483020)
XLA Ops:
  0.0 1.6 %pack.1 = (bf16[528,128]{1,0:T(8,128)(2,1)S(1)}, s32[8,128]{1,0:T(8,128)S(1)}) custom-call(s32[2]{0:T(128)} %bitcast.13, s32[2]{0:T(128)} %bitcast.14, bf16[512,128]{1,0:T(8,128)(2,1)} %bitcast.10), custom_call_target="tpu_custom_call" | custom-call | tf_op jit(solution)/shard_map/pack/pallas_call | solution.py:227
  1.6 4.0 %collective-permute-start.2 = (bf16[528,128]{1,0:T(8,128)(2,1)S(1)}, bf16[528,128]{1,0:T(8,128)(2,1)S(1)}, u32[]{:S(2)}, u32[]{:S(2)}) collective-permute-start(bf16[528,128]{1,0:T(8,128)(2,1)S(1)} %get-tuple-element.21.refs_0_), channel_id=1, source_target_pairs={{0,24},{8,16},{16,8},{24,0},{1,25},{9,17},{17,9},{25,1},{2,26},{10... | collective-permute-start | bytes 405512 | tf_op jit(solution)/shard_map/ppermute | solution.py:22
  5.6 0.5 %collective-permute-start.1 = (bf16[528,128]{1,0:T(8,128)(2,1)S(1)}, bf16[528,128]{1,0:T(8,128)(2,1)S(1)}, u32[]{:S(2)}, u32[]{:S(2)}) collective-permute-start(bf16[528,128]{1,0:T(8,128)(2,1)S(1)} %get-tuple-element.21.refs_0_), channel_id=1, source_target_pairs={{0,16},{8,24},{16,0},{24,8},{1,17},{9,25},{17,1},{25,9},{2,18},{10... | collective-permute-start | bytes 405512 | tf_op jit(solution)/shard_map/ppermute | solution.py:22
  6.1 0.1 collective-permute-start
  6.2 0.0 collective-permute-start.4
  6.2 4.1 %collective-permute-start.3 = (s32[8,128]{1,0:T(8,128)S(1)}, s32[8,128]{1,0:T(8,128)S(1)}, u32[]{:S(2)}, u32[]{:S(2)}) collective-permute-start(s32[8,128]{1,0:T(8,128)S(1)} %get-tuple-element.22.after.refs_4_), channel_id=1, source_target_pairs={{0,7},{1,2},{2,1},{3,4},{4,3},{5,6},{6,5},{7,0},{8,15},{9,10},{10,... | collective-permute-start | bytes 12296 | tf_op jit(solution)/shard_map/ppermute | solution.py:40
  11.0 2.1 %turn.1 = (bf16[256,4096]{1,0:T(8,128)(2,1)S(1)}, bf16[4096,256]{1,0:T(8,128)(2,1)S(1)}, f32[1,4096]{1,0:T(1,128)S(1)}) custom-call(s32[1]{0:T(128)} %bitcast.8.live, s32[8,128]{1,0:T(8,128)S(1)} %get-tuple-element.22.after.refs_4_, bf16[4096,256]{1,0:T(8,128)(2,1)} %bitcast.9, f32[1,4096]{1,0:T(1,128)} %bitcast.11, f32[1,4096]{1,0:T(1,128)} %bitcast.12), custom_call_target="tpu_custom_call" | custom-call | flops 536870912 | tf_op jit(solution)/shard_map/turn/pallas_call | solution.py:247
  13.1 0.0 collective-permute-done.4.refs_6_
  13.1 0.0 collective-permute-done.3.refs_5_
  13.1 0.0 collective-permute-done.2.refs_3_
  13.1 0.0 collective-permute-done.1.refs_2_
  13.1 0.0 collective-permute-done.refs_1_
  13.1 0.3 route.1
  13.4 2.4 %collective-permute-start.5 = (bf16[256,256]{1,0:T(8,128)(2,1)S(1)}, bf16[256,256]{1,0:T(8,128)(2,1)S(1)}, u32[]{:S(2)}, u32[]{:S(2)}) collective-permute-start(bf16[256,256]{1,0:T(8,128)(2,1)S(1)} %get-tuple-element.25), channel_id=1, source_target_pairs={{7,0},{2,1},{1,2},{4,3},{3,4},{6,5},{5,6},{0,7},{15,8},{10,9},{9,1... | collective-permute-start | bytes 393224 | tf_op jit(solution)/shard_map/ppermute | solution.py:46
  15.8 0.0 collective-permute-start.6
  15.8 0.7 %begin.1.early = f32[2,4096]{1,0:T(2,128)S(1)} custom-call(bf16[256,256]{1,0:T(8,128)(2,1)S(1)} %get-tuple-element.29.first, bf16[256,4096]{1,0:T(8,128)(2,1)S(1)} %get-tuple-element.27.turned), custom_call_target="tpu_custom_call" | custom-call | flops 536870912 | tf_op jit(solution)/shard_map/begin/pallas_call | solution.py:52
  16.6 4.1 %collective-permute-done.5.lower = bf16[256,256]{1,0:T(8,128)(2,1)S(1)} collective-permute-done((bf16[256,256]{1,0:T(8,128)(2,1)S(1)}, bf16[256,256]{1,0:T(8,128)(2,1)S(1)}, u32[]{:S(2)}, u32[]{:S(2)}) %collective-permute-start.5) | collective-permute-done | bytes 131104 | tf_op jit(solution)/shard_map/ppermute | solution.py:46
  20.6 0.0 collective-permute-done.6.upper
  20.6 2.0 %main.1 = (f32[256,256]{1,0:T(8,128)S(1)}, bf16[256,256]{1,0:T(8,128)(2,1)S(1)}, bf16[256,4096]{1,0:T(8,128)(2,1)S(1)}) custom-call(bf16[256,256]{1,0:T(8,128)(2,1)S(1)} %get-tuple-element.24.second, bf16[256,256]{1,0:T(8,128)(2,1)S(1)} %collective-permute-done.5.lower, bf16[256,256]{1,0:T(8,128)(2,1)S(1)} %collective-permute-done.6.upper, ...), custom_call_target="tpu_custom_call" | custom-call | flops 1073741824 | tf_op jit(solution)/shard_map/main/pallas_call | solution.py:52
  22.6 0.1 collective-permute-start.8
  22.7 1.5 %collective-permute-start.7 = (bf16[256,256]{1,0:T(8,128)(2,1)S(1)}, bf16[256,256]{1,0:T(8,128)(2,1)S(1)}, u32[]{:S(2)}, u32[]{:S(2)}) collective-permute-start(bf16[256,256]{1,0:T(8,128)(2,1)S(1)} %get-tuple-element.32), channel_id=1, source_target_pairs={{0,7},{1,2},{2,1},{3,4},{4,3},{5,6},{6,5},{7,0},{8,15},{9,10},{10,... | collective-permute-start | bytes 393224 | tf_op jit(solution)/shard_map/ppermute | solution.py:40
  24.1 0.7 %rest.1.refs_7_ = f32[256,256]{1,0:T(8,128)S(1)} custom-call(bf16[256,4096]{1,0:T(8,128)(2,1)S(1)} %get-tuple-element.30.scaled, bf16[4096,256]{1,0:T(8,128)(2,1)S(1)} %get-tuple-element.28.values), custom_call_target="tpu_custom_call" | custom-call | flops 536870912 | tf_op jit(solution)/shard_map/rest/pallas_call | solution.py:52
  24.8 0.0 collective-permute-done.8.refs_10_
  24.8 4.2 %collective-permute-done.7.refs_9_ = bf16[256,256]{1,0:T(8,128)(2,1)S(1)} collective-permute-done((bf16[256,256]{1,0:T(8,128)(2,1)S(1)}, bf16[256,256]{1,0:T(8,128)(2,1)S(1)}, u32[]{:S(2)}, u32[]{:S(2)}) %collective-permute-start.7) | collective-permute-done | bytes 131104 | tf_op jit(solution)/shard_map/ppermute | solution.py:40
  29.0 0.4 collect.1
  29.4 1.6 %collective-permute-start.9 = (bf16[512,128]{1,0:T(8,128)(2,1)S(1)}, bf16[512,128]{1,0:T(8,128)(2,1)S(1)}, u32[]{:S(2)}, u32[]{:S(2)}) collective-permute-start(bf16[512,128]{1,0:T(8,128)(2,1)S(1)} %get-tuple-element.34), channel_id=1, source_target_pairs={{8,0},{0,8},{24,16},{16,24},{9,1},{1,9},{25,17},{17,25},{10,2},{2,... | collective-permute-start | bytes 393224 | tf_op jit(solution)/shard_map/ppermute | solution.py:27
  31.0 1.0 %collective-permute-start.10 = (bf16[512,128]{1,0:T(8,128)(2,1)S(1)}, bf16[512,128]{1,0:T(8,128)(2,1)S(1)}, u32[]{:S(2)}, u32[]{:S(2)}) collective-permute-start(bf16[512,128]{1,0:T(8,128)(2,1)S(1)} %get-tuple-element.35), channel_id=1, source_target_pairs={{16,0},{24,8},{0,16},{8,24},{17,1},{25,9},{1,17},{9,25},{18,2},{26... | collective-permute-start | bytes 393224 | tf_op jit(solution)/shard_map/ppermute | solution.py:27
  32.0 1.0 %collective-permute-start.11 = (bf16[512,128]{1,0:T(8,128)(2,1)S(1)}, bf16[512,128]{1,0:T(8,128)(2,1)S(1)}, u32[]{:S(2)}, u32[]{:S(2)}) collective-permute-start(bf16[512,128]{1,0:T(8,128)(2,1)S(1)} %get-tuple-element.36), channel_id=1, source_target_pairs={{24,0},{16,8},{8,16},{0,24},{25,1},{17,9},{9,17},{1,25},{26,2},{18... | collective-permute-start | bytes 393224 | tf_op jit(solution)/shard_map/ppermute | solution.py:27
  33.0 2.3 %collective-permute-done.9.refs_1_ = bf16[512,128]{1,0:T(8,128)(2,1)S(1)} collective-permute-done((bf16[512,128]{1,0:T(8,128)(2,1)S(1)}, bf16[512,128]{1,0:T(8,128)(2,1)S(1)}, u32[]{:S(2)}, u32[]{:S(2)}) %collective-permute-start.9) | collective-permute-done | bytes 131104 | tf_op jit(solution)/shard_map/ppermute | solution.py:27
  35.3 3.7 %collective-permute-done.10.refs_2_ = bf16[512,128]{1,0:T(8,128)(2,1)S(1)} collective-permute-done((bf16[512,128]{1,0:T(8,128)(2,1)S(1)}, bf16[512,128]{1,0:T(8,128)(2,1)S(1)}, u32[]{:S(2)}, u32[]{:S(2)}) %collective-permute-start.10) | collective-permute-done | bytes 131104 | tf_op jit(solution)/shard_map/ppermute | solution.py:27
  39.0 0.0 collective-permute-done.11.refs_3_
  39.0 0.8 %add.1 = f32[512,128]{1,0:T(8,128)} custom-call(f32[512,128]{1,0:T(8,128)S(1)} %get-tuple-element.33.refs_0_, bf16[512,128]{1,0:T(8,128)(2,1)S(1)} %collective-permute-done.9.refs_1_, bf16[512,128]{1,0:T(8,128)(2,1)S(1)} %collective-permute-done.10.refs_2_, bf16[512,128]{1,0:T(8,128)(2,1)S(1)} %collective-permute-done.11.refs_3_), custom_call_target="tpu_custom_call" | custom-call | tf_op jit(solution)/shard_map/add/pallas_call | solution.py:52
Async XLA Ops:
  1.6 11.5 %collective-permute-start.2 = (bf16[528,128]{1,0:T(8,128)(2,1)S(1)}, bf16[528,128]{1,0:T(8,128)(2,1)S(1)}, u32[]{:S(2)}, u32[]{:S(2)}) collective-permute-start(bf16[528,128]{1,0:T(8,128)(2,1)S(1)} %get-tuple-element.21.refs_0_), channel_id=1, source_target_pairs={{0,24},{8,16},{16,8},{24,0},{1,25},{9,17},{17,9},{25,1},{2,26},{10... | collective-permute-start | bytes 405512 | tf_op jit(solution)/shard_map/ppermute | solution.py:22
  5.6 7.5 %collective-permute-start.1 = (bf16[528,128]{1,0:T(8,128)(2,1)S(1)}, bf16[528,128]{1,0:T(8,128)(2,1)S(1)}, u32[]{:S(2)}, u32[]{:S(2)}) collective-permute-start(bf16[528,128]{1,0:T(8,128)(2,1)S(1)} %get-tuple-element.21.refs_0_), channel_id=1, source_target_pairs={{0,16},{8,24},{16,0},{24,8},{1,17},{9,25},{17,1},{25,9},{2,18},{10... | collective-permute-start | bytes 405512 | tf_op jit(solution)/shard_map/ppermute | solution.py:22
  6.1 7.0 %collective-permute-start = (bf16[528,128]{1,0:T(8,128)(2,1)S(1)}, bf16[528,128]{1,0:T(8,128)(2,1)S(1)}, u32[]{:S(2)}, u32[]{:S(2)}) collective-permute-start(bf16[528,128]{1,0:T(8,128)(2,1)S(1)} %get-tuple-element.21.refs_0_), channel_id=1, source_target_pairs={{0,8},{8,0},{16,24},{24,16},{1,9},{9,1},{17,25},{25,17},{2,10},{10... | collective-permute-start | bytes 405512 | tf_op jit(solution)/shard_map/ppermute | solution.py:22
  6.2 6.9 %collective-permute-start.4 = (s32[8,128]{1,0:T(8,128)S(1)}, s32[8,128]{1,0:T(8,128)S(1)}, u32[]{:S(2)}, u32[]{:S(2)}) collective-permute-start(s32[8,128]{1,0:T(8,128)S(1)} %get-tuple-element.22.after.refs_4_), channel_id=1, source_target_pairs={{0,1},{1,0},{2,3},{3,2},{4,5},{5,4},{6,7},{7,6},{8,9},{9,8},{10,11... | collective-permute-start | bytes 12296 | tf_op jit(solution)/shard_map/ppermute | solution.py:40
  6.2 6.9 %collective-permute-start.3 = (s32[8,128]{1,0:T(8,128)S(1)}, s32[8,128]{1,0:T(8,128)S(1)}, u32[]{:S(2)}, u32[]{:S(2)}) collective-permute-start(s32[8,128]{1,0:T(8,128)S(1)} %get-tuple-element.22.after.refs_4_), channel_id=1, source_target_pairs={{0,7},{1,2},{2,1},{3,4},{4,3},{5,6},{6,5},{7,0},{8,15},{9,10},{10,... | collective-permute-start | bytes 12296 | tf_op jit(solution)/shard_map/ppermute | solution.py:40
  13.4 7.2 %collective-permute-start.5 = (bf16[256,256]{1,0:T(8,128)(2,1)S(1)}, bf16[256,256]{1,0:T(8,128)(2,1)S(1)}, u32[]{:S(2)}, u32[]{:S(2)}) collective-permute-start(bf16[256,256]{1,0:T(8,128)(2,1)S(1)} %get-tuple-element.25), channel_id=1, source_target_pairs={{7,0},{2,1},{1,2},{4,3},{3,4},{6,5},{5,6},{0,7},{15,8},{10,9},{9,1... | collective-permute-start | bytes 393224 | tf_op jit(solution)/shard_map/ppermute | solution.py:46
  15.8 4.8 %collective-permute-start.6 = (bf16[256,256]{1,0:T(8,128)(2,1)S(1)}, bf16[256,256]{1,0:T(8,128)(2,1)S(1)}, u32[]{:S(2)}, u32[]{:S(2)}) collective-permute-start(bf16[256,256]{1,0:T(8,128)(2,1)S(1)} %get-tuple-element.26), channel_id=1, source_target_pairs={{1,0},{0,1},{3,2},{2,3},{5,4},{4,5},{7,6},{6,7},{9,8},{8,9},{11,10... | collective-permute-start | bytes 393224 | tf_op jit(solution)/shard_map/ppermute | solution.py:46
  22.6 2.2 %collective-permute-start.8 = (bf16[256,256]{1,0:T(8,128)(2,1)S(1)}, bf16[256,256]{1,0:T(8,128)(2,1)S(1)}, u32[]{:S(2)}, u32[]{:S(2)}) collective-permute-start(bf16[256,256]{1,0:T(8,128)(2,1)S(1)} %get-tuple-element.32), channel_id=1, source_target_pairs={{0,1},{1,0},{2,3},{3,2},{4,5},{5,4},{6,7},{7,6},{8,9},{9,8},{10,11... | collective-permute-start | bytes 393224 | tf_op jit(solution)/shard_map/ppermute | solution.py:40
  22.7 6.4 %collective-permute-start.7 = (bf16[256,256]{1,0:T(8,128)(2,1)S(1)}, bf16[256,256]{1,0:T(8,128)(2,1)S(1)}, u32[]{:S(2)}, u32[]{:S(2)}) collective-permute-start(bf16[256,256]{1,0:T(8,128)(2,1)S(1)} %get-tuple-element.32), channel_id=1, source_target_pairs={{0,7},{1,2},{2,1},{3,4},{4,3},{5,6},{6,5},{7,0},{8,15},{9,10},{10,... | collective-permute-start | bytes 393224 | tf_op jit(solution)/shard_map/ppermute | solution.py:40
  29.4 5.9 %collective-permute-start.9 = (bf16[512,128]{1,0:T(8,128)(2,1)S(1)}, bf16[512,128]{1,0:T(8,128)(2,1)S(1)}, u32[]{:S(2)}, u32[]{:S(2)}) collective-permute-start(bf16[512,128]{1,0:T(8,128)(2,1)S(1)} %get-tuple-element.34), channel_id=1, source_target_pairs={{8,0},{0,8},{24,16},{16,24},{9,1},{1,9},{25,17},{17,25},{10,2},{2,... | collective-permute-start | bytes 393224 | tf_op jit(solution)/shard_map/ppermute | solution.py:27
  31.0 7.9 %collective-permute-start.10 = (bf16[512,128]{1,0:T(8,128)(2,1)S(1)}, bf16[512,128]{1,0:T(8,128)(2,1)S(1)}, u32[]{:S(2)}, u32[]{:S(2)}) collective-permute-start(bf16[512,128]{1,0:T(8,128)(2,1)S(1)} %get-tuple-element.35), channel_id=1, source_target_pairs={{16,0},{24,8},{0,16},{8,24},{17,1},{25,9},{1,17},{9,25},{18,2},{26... | collective-permute-start | bytes 393224 | tf_op jit(solution)/shard_map/ppermute | solution.py:27
  32.0 7.0 %collective-permute-start.11 = (bf16[512,128]{1,0:T(8,128)(2,1)S(1)}, bf16[512,128]{1,0:T(8,128)(2,1)S(1)}, u32[]{:S(2)}, u32[]{:S(2)}) collective-permute-start(bf16[512,128]{1,0:T(8,128)(2,1)S(1)} %get-tuple-element.36), channel_id=1, source_target_pairs={{24,0},{16,8},{8,16},{0,24},{25,1},{17,9},{9,17},{1,25},{26,2},{18... | collective-permute-start | bytes 393224 | tf_op jit(solution)/shard_map/ppermute | solution.py:27
